TPU v7x, 32 devices: a whole 2x2x4 slice. The times are simulated.
32 devices in a mesh: fsdp: 4 (over y, core), grp: 8 (over z, x).
Axes of the slice: x: 2, y: 2, z: 4, core: 2. Of those that a mesh axis runs over, the one named last changes fastest.
Arguments:
- grad: bfloat16 [8, 512, 2048], P('grp', 'fsdp'), may hold values from -30 to 30
- table: int32 [8, 4], P('grp'), may hold values from 0 to 3, each once within a row
- left_stat: bfloat16 [8, 4, 512, 512], P('grp', 'fsdp'), may hold values from -4 to 4, as said below
- right_stat: bfloat16 [8, 4, 512, 512], P('grp', 'fsdp'), may hold values from -4 to 4, as said below
- left_basis: bfloat16 [8, 4, 512, 512], P('grp', 'fsdp'), may hold values from -4 to 4, as said below
- right_basis: bfloat16 [8, 4, 512, 512], P('grp', 'fsdp'), may hold values from -4 to 4, as said below
- row_moment: float32 [8, 4, 512], P('grp', 'fsdp'), may hold values from 0.05 to 1
- col_moment: float32 [8, 4, 512], P('grp', 'fsdp'), may hold values from 0.05 to 1
Outputs:
- update: bfloat16 [8, 512, 2048], P('grp', 'fsdp')
- row_next: float32 [8, 4, 512], P('grp', 'fsdp')
- col_next: float32 [8, 4, 512], P('grp', 'fsdp')
Inputs may be any that keep to these rules, and one draw needn't show every extreme that they name: Each row of table lists every owner 0 to 3 once. `left_stat`: symmetric with a dominant diagonal. `right_stat`: symmetric with a dominant diagonal. `left_basis`: nonsingular. `right_basis`: nonsingular.
All inputs are finite; a program needn't handle non-finite values.
Results may differ from a plain program's by a relative error of at most 0.01.
Values may be sent and summed in bfloat16 or wider, within the bound.
A program may use at most 64 MiB of HBM per device.

v0:
```python
import functools
import jax
import jax.numpy as jnp
from jax import lax
from jax.experimental import pallas as pl
from jax.experimental.pallas import tpu as pltpu
from jax.sharding import PartitionSpec as P

DECAY_STAT = 0.95
DECAY_MOMENT = 0.95
CLIP_RMS = 0.5
EPSILON = 1e-08
OUTER = 128
INNER = 32
PANEL = 16

NN = (((1,), (0,)), ((), ()))
NT = (((1,), (1,)), ((), ()))
TN = (((0,), (0,)), ((), ()))
MESH = pl.DeviceIdType.MESH


def mm(a, b, dims=NN):
    return lax.dot_general(a, b, dims, preferred_element_type=jnp.float32)


def mm_high(a, b, dims=NN):
    return lax.dot_general(a, b, dims, preferred_element_type=jnp.float32, precision=lax.Precision.HIGHEST)


def split(a):
    high = a.astype(jnp.bfloat16)
    return high, (a - high.astype(jnp.float32)).astype(jnp.bfloat16)


def mm_split(a, b, dims=NN):
    return mm(a[0], b[0], dims) + (mm(a[0], b[1], dims) + mm(a[1], b[0], dims))


def eliminate(pack):
    lane = lax.broadcasted_iota(jnp.int32, pack.shape, 1)
    row = lax.broadcasted_iota(jnp.int32, pack.shape, 0)
    low = lane < 2 * INNER
    scale = jnp.ones_like(pack)
    done = []
    rest = pack
    for start in range(0, INNER, PANEL):
        shape = rest.shape
        below = lax.broadcasted_iota(jnp.int32, shape, 0)
        half = low[: shape[0]]
        columns = [
            jnp.where(
                half,
                jnp.broadcast_to(rest[:, j : j + 1], shape),
                jnp.broadcast_to(rest[:, 2 * INNER + j : 2 * INNER + j + 1], shape),
            )
            for j in range(start, start + PANEL)
        ]
        head_scale = jnp.ones((PANEL, shape[1]), jnp.float32)
        for p in range(PANEL):
            pivot = columns[p][p : p + 1, :]
            root = lax.rsqrt(pivot)
            inverse = root * root
            factor = jnp.where(below > p, columns[p], 0.0) * inverse
            for q in range(p + 1, PANEL):
                columns[q] = columns[q] - factor * columns[q][p : p + 1, :]
            rest = rest - factor * rest[p : p + 1, :]
            head_scale = jnp.where(below[:PANEL] == p, root, head_scale)
        done.append(rest[:PANEL] * head_scale)
        rest = rest[PANEL:]
    return jnp.concatenate(done, axis=0)


def inverse_factors(grams, work):
    row = lax.broadcasted_iota(jnp.int32, (OUTER, OUTER), 0)
    col = lax.broadcasted_iota(jnp.int32, (OUTER, OUTER), 1)
    eye = jnp.where(row == col, 1.0, 0.0)
    for c in range(2):
        work[c, :, :OUTER] = grams[c]
        work[c, :, OUTER:] = eye
    small_row = lax.broadcasted_iota(jnp.int32, (INNER, OUTER), 0)
    lane = lax.broadcasted_iota(jnp.int32, (INNER, OUTER), 1)
    small_eye = jnp.where((lane == small_row + INNER) | (lane == small_row + 3 * INNER), 1.0, 0.0)
    for b in range(OUTER // INNER):
        rows = pl.ds(b * INNER, INNER)
        left = work[0, rows, :OUTER]
        right = work[1, rows, :OUTER]
        if b:
            left = pltpu.roll(left, OUTER - b * INNER, 1)
        shift = (2 * INNER - b * INNER) % OUTER
        if shift:
            right = pltpu.roll(right, shift, 1)
        pack = jnp.where(lane < INNER, left, small_eye)
        pack = jnp.where((lane >= 2 * INNER) & (lane < 3 * INNER), right, pack)
        pack = eliminate(pack)
        for c in range(2):
            factor = pltpu.roll(pack, OUTER - INNER if c == 0 else INNER, 1)[:, :INNER]
            solved = mm_split(split(factor), split(work[c, rows, :]))
            work[c, rows, :] = solved
            if (b + 1) * INNER < OUTER:
                tail = pl.ds((b + 1) * INNER, OUTER - (b + 1) * INNER)
                high, low = split(solved)
                cut = slice((b + 1) * INNER, OUTER)
                work[c, tail, :] = work[c, tail, :] - mm_split((high[:, cut], low[:, cut]), (high, low), TN)
    return [work[c, :, OUTER:] for c in range(2)]


def partners(owners):
    return [(chip, core) for chip in range(owners // 2 - 1, -1, -1) for core in (1, 0) if chip or core]


def soap_kernel(
    groups, table_ref, grad_ref, ls_hbm, rs_hbm, lb_hbm, rb_hbm, rm_ref, cm_ref, out_ref, rn_ref, cn_ref,
    stat_ref, basis_ref, send_ref, block_ref, back_ref, ret_ref, sums_ref, totals_ref, part_ref,
    x_ref, q_ref, work,
    load_sem, stripe_send, stripe_recv, sum_send, sum_recv, total_send, total_recv, slab_send, slab_recv,
):
    owners, my_rows, order = send_ref.shape
    me = lax.axis_index("fsdp")
    group = lax.axis_index("grp")
    offsets = partners(owners)

    def peer(offset):
        return lax.rem(me // 2 + offset[0], owners // 2) * 2 + lax.rem(me + offset[1], 2)

    def group_peer(step):
        return lax.rem(group + step, groups)

    loads = []
    for i, (source, target) in enumerate(
        ((lb_hbm, basis_ref.at[0]), (ls_hbm, stat_ref.at[0]), (rb_hbm, basis_ref.at[1]), (rs_hbm, stat_ref.at[1]))
    ):
        loads.append(pltpu.make_async_copy(source, target, load_sem.at[i]))
        loads[-1].start()
    barrier = pltpu.get_barrier_semaphore()
    for offset in offsets:
        pl.semaphore_signal(barrier, inc=1, device_id={"fsdp": peer(offset)}, device_id_type=MESH)
    for step in range(1, groups):
        pl.semaphore_signal(barrier, inc=1, device_id={"grp": group_peer(step)}, device_id_type=MESH)

    def pick(owner_of, pieces):
        chosen = jnp.zeros(pieces[0].shape, jnp.float32)
        for owner, piece in zip(owner_of, pieces):
            chosen = jnp.where(jnp.full(piece.shape, owner[0], jnp.int32) == owner[1], piece.astype(jnp.float32), chosen)
        return chosen.astype(jnp.bfloat16)

    def stripe(owner):
        pieces = [grad_ref[:, j * order : (j + 1) * order] for j in range(owners)]
        return pick([(table_ref[0, j], owner) for j in range(owners)], pieces)

    for offset in offsets:
        owner = peer(offset)
        send_ref[owner] = stripe(owner)
    my_slab = pl.ds(pl.multiple_of(me * my_rows, my_rows), my_rows)
    block_ref[my_slab, :] = stripe(me)
    local = jnp.zeros((1, order), jnp.float32)
    for j in range(owners):
        piece = grad_ref[:, j * order : (j + 1) * order].astype(jnp.float32)
        local = local + jnp.sum(piece * piece, axis=0, keepdims=True)
    local = jnp.broadcast_to(jnp.sum(local, axis=1, keepdims=True), sums_ref.shape[1:])
    part_ref[0] = local
    sums_ref[me] = local
    pl.semaphore_wait(barrier, owners - 1 + groups - 1)

    sum_copies, stripe_copies, total_copies, slab_copies = [], [], [], []
    for i, offset in enumerate(offsets):
        sum_copies.append(
            pltpu.make_async_remote_copy(
                src_ref=part_ref.at[0], dst_ref=sums_ref.at[me], send_sem=sum_send.at[i], recv_sem=sum_recv.at[i],
                device_id={"fsdp": peer(offset)}, device_id_type=MESH,
            )
        )
        sum_copies[-1].start()
    for i, offset in enumerate(offsets):
        stripe_copies.append(
            pltpu.make_async_remote_copy(
                src_ref=send_ref.at[peer(offset)], dst_ref=block_ref.at[my_slab, :],
                send_sem=stripe_send.at[i], recv_sem=stripe_recv.at[i],
                device_id={"fsdp": peer(offset)}, device_id_type=MESH,
            )
        )
        stripe_copies[-1].start()
    loads[0].wait()
    loads[1].wait()
    x_ref[0] = mm(basis_ref[0], stat_ref[0], TN)
    for copy in sum_copies:
        copy.wait_recv()
    matrix_sum = sums_ref[0]
    for i in range(1, owners):
        matrix_sum = matrix_sum + sums_ref[i]
    part_ref[1] = matrix_sum
    totals_ref[group] = matrix_sum
    loads[2].wait()
    loads[3].wait()
    for step in range(1, groups):
        total_copies.append(
            pltpu.make_async_remote_copy(
                src_ref=part_ref.at[1], dst_ref=totals_ref.at[group],
                send_sem=total_send.at[step - 1], recv_sem=total_recv.at[step - 1],
                device_id={"grp": group_peer(step)}, device_id_type=MESH,
            )
        )
        total_copies[-1].start()
    x_ref[1] = mm(basis_ref[1], stat_ref[1], TN)
    for copy in total_copies:
        copy.wait_recv()
    total = totals_ref[0]
    for i in range(1, groups):
        total = total + totals_ref[i]
    count = float(groups * owners * order * order)
    clip = (CLIP_RMS / jnp.sqrt(total / count + 1e-06))[:1, :1]
    weight = (1.0 - DECAY_STAT) * clip * clip
    for copy in stripe_copies:
        copy.wait_recv()
    g = block_ref[...]
    for c, dims in enumerate((NT, TN)):
        high, low = split(mm(g, g, dims))
        product = mm(basis_ref[c], high, TN) + mm(basis_ref[c], low, TN)
        x_ref[c] = DECAY_STAT * x_ref[c] + weight * product
    for k in range(order // OUTER):
        rows = pl.ds(k * OUTER, OUTER)
        grams = []
        for c in range(2):
            grams.append(mm_high(x_ref[c, rows, :], x_ref[c, rows, :], NT))
        factors = inverse_factors(grams, work)
        for c in range(2):
            block = mm_split(split(factors[c]), split(x_ref[c, rows, :]))
            q_ref[c, rows, :] = block.astype(jnp.bfloat16)
            if (k + 1) * OUTER < order:
                parts = split(block)
                near, far = (k + 1) * OUTER, (k + 2) * OUTER
                for tail in (pl.ds(near, OUTER), pl.ds(far, order - far)):
                    if tail.size:
                        along = mm_split(split(x_ref[c, tail, :]), parts, NT)
                        x_ref[c, tail, :] = x_ref[c, tail, :] - mm_split(split(along), parts)
    half = mm(q_ref[0], g).astype(jnp.bfloat16)
    rotated = clip * mm(half, q_ref[1], NT)
    square = rotated * rotated
    lanes = 128
    mean_row = jnp.broadcast_to(jnp.mean(square, axis=1, keepdims=True), (order, lanes))
    mean_col = jnp.mean(square, axis=0, keepdims=True)
    row_next = DECAY_MOMENT * jnp.broadcast_to(rm_ref[...], (lanes, order)) + (1.0 - DECAY_MOMENT) * mean_row.T
    col_next = DECAY_MOMENT * cm_ref[...] + (1.0 - DECAY_MOMENT) * mean_col
    rn_ref[...] = row_next[:1]
    cn_ref[...] = col_next
    second = row_next.T[:, :1] * col_next / jnp.mean(row_next[:1])
    normed = (rotated / (jnp.sqrt(second) + EPSILON)).astype(jnp.bfloat16)
    back_ref[...] = mm(q_ref[0], normed, TN).astype(jnp.bfloat16)
    for copy in stripe_copies:
        copy.wait_send()

    def slab(owner):
        rows = pl.ds(pl.multiple_of(owner * my_rows, my_rows), my_rows)
        return mm(back_ref[rows, :], q_ref[1]).astype(jnp.bfloat16)

    for i, offset in enumerate(offsets):
        send_ref[peer(offset)] = slab(peer(offset))
        slab_copies.append(
            pltpu.make_async_remote_copy(
                src_ref=send_ref.at[peer(offset)], dst_ref=ret_ref.at[me],
                send_sem=slab_send.at[i], recv_sem=slab_recv.at[i],
                device_id={"fsdp": peer(offset)}, device_id_type=MESH,
            )
        )
        if i:
            slab_copies[i - 1].start()
    ret_ref[me] = slab(me)
    slab_copies[-1].start()
    for copy in slab_copies:
        copy.wait_recv()
    for j in range(owners):
        out_ref[:, j * order : (j + 1) * order] = pick([(table_ref[0, j], o) for o in range(owners)], [ret_ref[o] for o in range(owners)])
    for copy in sum_copies + total_copies + slab_copies:
        copy.wait_send()


def shards(grad, table, left_stat, right_stat, left_basis, right_basis, row_moment, col_moment):
    order = left_stat.shape[-1]
    owners = lax.axis_size("fsdp")
    groups = lax.axis_size("grp")
    my_rows = grad.shape[1]
    vmem = pl.BlockSpec(memory_space=pltpu.VMEM)
    hbm = pl.BlockSpec(memory_space=pl.ANY)
    dma = pltpu.SemaphoreType.DMA
    update, row_next, col_next = pl.pallas_call(
        functools.partial(soap_kernel, groups),
        out_shape=(
            jax.ShapeDtypeStruct((my_rows, owners * order), jnp.bfloat16),
            jax.ShapeDtypeStruct((1, order), jnp.float32),
            jax.ShapeDtypeStruct((1, order), jnp.float32),
        ),
        in_specs=[pl.BlockSpec(memory_space=pltpu.SMEM), vmem, hbm, hbm, hbm, hbm, vmem, vmem],
        out_specs=(vmem, vmem, vmem),
        scratch_shapes=[
            pltpu.VMEM((2, order, order), jnp.bfloat16),
            pltpu.VMEM((2, order, order), jnp.bfloat16),
            pltpu.VMEM((owners, my_rows, order), jnp.bfloat16),
            pltpu.VMEM((order, order), jnp.bfloat16),
            pltpu.VMEM((order, order), jnp.bfloat16),
            pltpu.VMEM((owners, my_rows, order), jnp.bfloat16),
            pltpu.VMEM((owners, 8, 128), jnp.float32),
            pltpu.VMEM((groups, 8, 128), jnp.float32),
            pltpu.VMEM((2, 8, 128), jnp.float32),
            pltpu.VMEM((2, order, order), jnp.float32),
            pltpu.VMEM((2, order, order), jnp.bfloat16),
            pltpu.VMEM((2, OUTER, 2 * OUTER), jnp.float32),
            dma((4,)),
            dma((owners - 1,)),
            dma((owners - 1,)),
            dma((owners - 1,)),
            dma((owners - 1,)),
            dma((groups - 1,)),
            dma((groups - 1,)),
            dma((owners - 1,)),
            dma((owners - 1,)),
        ],
        compiler_params=pltpu.CompilerParams(
            collective_id=0, has_side_effects=True, vmem_limit_bytes=48 * 1024 * 1024
        ),
        name="soap",
    )(
        table, grad[0], left_stat[0, 0], right_stat[0, 0], left_basis[0, 0], right_basis[0, 0],
        row_moment[0], col_moment[0],
    )
    return (update[None], row_next[None], col_next[None])


def solution(mesh):
    in_specs = (
        P("grp", "fsdp", None),
        P("grp", None),
        P("grp", "fsdp", None, None),
        P("grp", "fsdp", None, None),
        P("grp", "fsdp", None, None),
        P("grp", "fsdp", None, None),
        P("grp", "fsdp", None),
        P("grp", "fsdp", None),
    )
    out_specs = (P("grp", "fsdp", None), P("grp", "fsdp", None), P("grp", "fsdp", None))
    return jax.shard_map(shards, mesh=mesh, in_specs=in_specs, out_specs=out_specs, check_vma=False)
```

profile of v0, /device:TPU:0, one launch (start us, length us, event | category | flops | bytes accessed | tf_op | source)
XLA Modules:
  0.0 59.8 jit_solution(14026797898577066584)
XLA Ops:
  0.6 0.0 copy-start.6
  0.6 0.0 copy-start.5
  0.7 0.0 copy-start.7
  0.7 0.7 %copy-done.6 = f32[1,1,512]{2,1,0:T(1,128)S(1)} copy-done((f32[1,1,512]{2,1,0:T(1,128)S(1)}, f32[1,1,512]{2,1,0:T(1,128)}, u32[]{:S(2)}) %copy-start.6) | copy-done | bytes 2072
  1.3 0.0 copy-done.5
  1.3 0.0 copy-done.7
  1.3 0.0 copy-start
  1.3 1.0 %copy-done = bf16[1,128,2048]{2,1,0:T(8,128)(2,1)S(1)} copy-done((bf16[1,128,2048]{2,1,0:T(8,128)(2,1)S(1)}, bf16[1,128,2048]{2,1,0:T(8,128)(2,1)}, u32[]{:S(2)}) %copy-start) | copy-done | bytes 524312
  2.4 0.0 copy-start.1
  2.4 1.0 %copy-done.1 = bf16[1,1,512,512]{3,2,1,0:T(8,128)(2,1)S(1)} copy-done((bf16[1,1,512,512]{3,2,1,0:T(8,128)(2,1)S(1)}, bf16[1,1,512,512]{3,2,1,0:T(8,128)(2,1)}, u32[]{:S(2)}) %copy-start.1) | copy-done | bytes 524312
  3.4 0.0 copy-start.2
  3.4 1.0 %copy-done.2 = bf16[1,1,512,512]{3,2,1,0:T(8,128)(2,1)S(1)} copy-done((bf16[1,1,512,512]{3,2,1,0:T(8,128)(2,1)S(1)}, bf16[1,1,512,512]{3,2,1,0:T(8,128)(2,1)}, u32[]{:S(2)}) %copy-start.2) | copy-done | bytes 524312
  4.5 0.0 copy-start.3
  4.5 1.0 %copy-done.3 = bf16[1,1,512,512]{3,2,1,0:T(8,128)(2,1)S(1)} copy-done((bf16[1,1,512,512]{3,2,1,0:T(8,128)(2,1)S(1)}, bf16[1,1,512,512]{3,2,1,0:T(8,128)(2,1)}, u32[]{:S(2)}) %copy-start.3) | copy-done | bytes 524312
  5.5 0.0 copy-start.4
  5.5 1.0 %copy-done.4 = bf16[1,1,512,512]{3,2,1,0:T(8,128)(2,1)S(1)} copy-done((bf16[1,1,512,512]{3,2,1,0:T(8,128)(2,1)S(1)}, bf16[1,1,512,512]{3,2,1,0:T(8,128)(2,1)}, u32[]{:S(2)}) %copy-start.4) | copy-done | bytes 524312
  6.5 51.3 %soap.1 = (bf16[128,2048]{1,0:T(8,128)(2,1)S(1)}, f32[1,512]{1,0:T(1,128)S(1)}, f32[1,512]{1,0:T(1,128)S(1)}) custom-call(s32[1,4]{1,0:T(1,128)S(1)} %copy-done.7, bf16[128,2048]{1,0:T(8,128)(2,1)S(1)} %bitcast.11, bf16[512,512]{1,0:T(8,128)(2,1)S(1)} %bitcast.12, bf16[512,512]{1,0:T(8,128)(2,1)S(1)} %bitcast.13, bf16[512,512]{1,0:T(8,128)(2,1)S(1)} %bitcast.14, ...), custom_call_target="tpu_custom_call" | custom-call | tf_op jit(solution)/shard_map/soap/pallas_call | solution.py:285
  57.9 0.8 %copy.14 = bf16[1,128,2048]{2,1,0:T(8,128)(2,1)} copy(bf16[1,128,2048]{2,1,0:T(8,128)(2,1)S(1)} %bitcast.10) | data formatting | bytes 1048576
  58.7 0.6 copy.15
  59.2 0.6 copy.16
Async XLA Ops:
  0.6 0.7 %copy-start.6 = (f32[1,1,512]{2,1,0:T(1,128)S(1)}, f32[1,1,512]{2,1,0:T(1,128)}, u32[]{:S(2)}) copy-start(f32[1,1,512]{2,1,0:T(1,128)} %param.15) | copy-start | bytes 6148
  0.6 0.7 %copy-start.5 = (f32[1,1,512]{2,1,0:T(1,128)S(1)}, f32[1,1,512]{2,1,0:T(1,128)}, u32[]{:S(2)}) copy-start(f32[1,1,512]{2,1,0:T(1,128)} %param.14) | copy-start | bytes 6148
  0.7 0.7 %copy-start.7 = (s32[1,4]{1,0:T(1,128)S(1)}, s32[1,4]{1,0:T(1,128)}, u32[]{:S(2)}) copy-start(s32[1,4]{1,0:T(1,128)} %table_ref.1) | copy-start | bytes 52
  1.3 1.0 %copy-start = (bf16[1,128,2048]{2,1,0:T(8,128)(2,1)S(1)}, bf16[1,128,2048]{2,1,0:T(8,128)(2,1)}, u32[]{:S(2)}) copy-start(bf16[1,128,2048]{2,1,0:T(8,128)(2,1)} %param.8) | copy-start | bytes 1572868
  2.4 1.0 %copy-start.1 = (bf16[1,1,512,512]{3,2,1,0:T(8,128)(2,1)S(1)}, bf16[1,1,512,512]{3,2,1,0:T(8,128)(2,1)}, u32[]{:S(2)}) copy-start(bf16[1,1,512,512]{3,2,1,0:T(8,128)(2,1)} %param.10) | copy-start | bytes 1572868
  3.4 1.0 %copy-start.2 = (bf16[1,1,512,512]{3,2,1,0:T(8,128)(2,1)S(1)}, bf16[1,1,512,512]{3,2,1,0:T(8,128)(2,1)}, u32[]{:S(2)}) copy-start(bf16[1,1,512,512]{3,2,1,0:T(8,128)(2,1)} %param.11) | copy-start | bytes 1572868
  4.5 1.0 %copy-start.3 = (bf16[1,1,512,512]{3,2,1,0:T(8,128)(2,1)S(1)}, bf16[1,1,512,512]{3,2,1,0:T(8,128)(2,1)}, u32[]{:S(2)}) copy-start(bf16[1,1,512,512]{3,2,1,0:T(8,128)(2,1)} %param.12) | copy-start | bytes 1572868
  5.5 1.0 %copy-start.4 = (bf16[1,1,512,512]{3,2,1,0:T(8,128)(2,1)S(1)}, bf16[1,1,512,512]{3,2,1,0:T(8,128)(2,1)}, u32[]{:S(2)}) copy-start(bf16[1,1,512,512]{3,2,1,0:T(8,128)(2,1)} %param.13) | copy-start | bytes 1572868
where the time goes:
time: 60.2 us; the launch traced here: 59.8 us
  Pallas kernels  51.3 us (85%)
  local copies, waits for them, and re-layouts  7.83 us (13%)
  between operations  0.67 us (1%)
    pallas_call x1, Pallas kernels, shards(): pl.pallas_call(functools.partial(soap_kernel, groups), out_shape=(jax.Sha...  51.3 us
    unnamed x19, local copies, waits for them, and re-layouts  7.83 us

commit v1 on v0

--- a/solution.py
+++ b/solution.py
@@ -110,7 +110,8 @@
 
 
 def soap_kernel(
-    groups, table_ref, grad_ref, ls_hbm, rs_hbm, lb_hbm, rb_hbm, rm_ref, cm_ref, out_ref, rn_ref, cn_ref,
+    groups, table_hbm, grad_hbm, ls_hbm, rs_hbm, lb_hbm, rb_hbm, rm_hbm, cm_hbm, out_ref, rn_ref, cn_ref,
+    table_ref, grad_ref, rm_ref, cm_ref,
     stat_ref, basis_ref, send_ref, block_ref, back_ref, ret_ref, sums_ref, totals_ref, part_ref,
     x_ref, q_ref, work,
     load_sem, stripe_send, stripe_recv, sum_send, sum_recv, total_send, total_recv, slab_send, slab_recv,
@@ -127,26 +128,31 @@
         return lax.rem(group + step, groups)
 
     loads = []
-    for i, (source, target) in enumerate(
-        ((lb_hbm, basis_ref.at[0]), (ls_hbm, stat_ref.at[0]), (rb_hbm, basis_ref.at[1]), (rs_hbm, stat_ref.at[1]))
-    ):
-        loads.append(pltpu.make_async_copy(source, target, load_sem.at[i]))
+
+    def load(source, target):
+        loads.append(pltpu.make_async_copy(source, target, load_sem.at[len(loads)]))
         loads[-1].start()
+        return loads[-1]
+
+    gradient = [load(table_hbm, table_ref)]
+    for j in range(owners):
+        gradient.append(load(grad_hbm.at[:, pl.ds(j * order, order)], grad_ref.at[j]))
+    left = [load(lb_hbm, basis_ref.at[0]), load(ls_hbm, stat_ref.at[0])]
+    right = [load(rb_hbm, basis_ref.at[1]), load(rs_hbm, stat_ref.at[1])]
+    moments = [load(rm_hbm, rm_ref), load(cm_hbm, cm_ref)]
     barrier = pltpu.get_barrier_semaphore()
     for offset in offsets:
         pl.semaphore_signal(barrier, inc=1, device_id={"fsdp": peer(offset)}, device_id_type=MESH)
     for step in range(1, groups):
         pl.semaphore_signal(barrier, inc=1, device_id={"grp": group_peer(step)}, device_id_type=MESH)
-
-    def pick(owner_of, pieces):
-        chosen = jnp.zeros(pieces[0].shape, jnp.float32)
-        for owner, piece in zip(owner_of, pieces):
-            chosen = jnp.where(jnp.full(piece.shape, owner[0], jnp.int32) == owner[1], piece.astype(jnp.float32), chosen)
-        return chosen.astype(jnp.bfloat16)
+    for copy in gradient:
+        copy.wait()
 
     def stripe(owner):
-        pieces = [grad_ref[:, j * order : (j + 1) * order] for j in range(owners)]
-        return pick([(table_ref[0, j], owner) for j in range(owners)], pieces)
+        column = jnp.int32(0)
+        for j in range(1, owners):
+            column = jnp.where(table_ref[0, j] == owner, j, column)
+        return grad_ref[column]
 
     for offset in offsets:
         owner = peer(offset)
@@ -155,7 +161,7 @@
     block_ref[my_slab, :] = stripe(me)
     local = jnp.zeros((1, order), jnp.float32)
     for j in range(owners):
-        piece = grad_ref[:, j * order : (j + 1) * order].astype(jnp.float32)
+        piece = grad_ref[j].astype(jnp.float32)
         local = local + jnp.sum(piece * piece, axis=0, keepdims=True)
     local = jnp.broadcast_to(jnp.sum(local, axis=1, keepdims=True), sums_ref.shape[1:])
     part_ref[0] = local
@@ -180,8 +186,8 @@
             )
         )
         stripe_copies[-1].start()
-    loads[0].wait()
-    loads[1].wait()
+    for copy in left:
+        copy.wait()
     x_ref[0] = mm(basis_ref[0], stat_ref[0], TN)
     for copy in sum_copies:
         copy.wait_recv()
@@ -190,8 +196,10 @@
         matrix_sum = matrix_sum + sums_ref[i]
     part_ref[1] = matrix_sum
     totals_ref[group] = matrix_sum
-    loads[2].wait()
-    loads[3].wait()
+    for copy in right:
+        copy.wait()
+    for copy in moments:
+        copy.wait()
     for step in range(1, groups):
         total_copies.append(
             pltpu.make_async_remote_copy(
@@ -202,6 +210,10 @@
         )
         total_copies[-1].start()
     x_ref[1] = mm(basis_ref[1], stat_ref[1], TN)
+    for copy in stripe_copies:
+        copy.wait_recv()
+    g = block_ref[...]
+    grams = [split(mm(g, g, dims)) for dims in (NT, TN)]
     for copy in total_copies:
         copy.wait_recv()
     total = totals_ref[0]
@@ -210,11 +222,8 @@
     count = float(groups * owners * order * order)
     clip = (CLIP_RMS / jnp.sqrt(total / count + 1e-06))[:1, :1]
     weight = (1.0 - DECAY_STAT) * clip * clip
-    for copy in stripe_copies:
-        copy.wait_recv()
-    g = block_ref[...]
-    for c, dims in enumerate((NT, TN)):
-        high, low = split(mm(g, g, dims))
+    for c in range(2):
+        high, low = grams[c]
         product = mm(basis_ref[c], high, TN) + mm(basis_ref[c], low, TN)
         x_ref[c] = DECAY_STAT * x_ref[c] + weight * product
     for k in range(order // OUTER):
@@ -269,9 +278,20 @@
     for copy in slab_copies:
         copy.wait_recv()
     for j in range(owners):
-        out_ref[:, j * order : (j + 1) * order] = pick([(table_ref[0, j], o) for o in range(owners)], [ret_ref[o] for o in range(owners)])
+        out_ref[:, j * order : (j + 1) * order] = ret_ref[table_ref[0, j]]
     for copy in sum_copies + total_copies + slab_copies:
         copy.wait_send()
+
+
+def store_kernel(update_ref, rn_ref, cn_ref, update_hbm, rn_hbm, cn_hbm, sem):
+    copies = [
+        pltpu.make_async_copy(source, target, sem.at[i])
+        for i, (source, target) in enumerate(((update_ref, update_hbm), (rn_ref, rn_hbm), (cn_ref, cn_hbm)))
+    ]
+    for copy in copies:
+        copy.start()
+    for copy in copies:
+        copy.wait()
 
 
 def shards(grad, table, left_stat, right_stat, left_basis, right_basis, row_moment, col_moment):
@@ -280,7 +300,7 @@
     groups = lax.axis_size("grp")
     my_rows = grad.shape[1]
     vmem = pl.BlockSpec(memory_space=pltpu.VMEM)
-    hbm = pl.BlockSpec(memory_space=pl.ANY)
+    hbm = pl.BlockSpec(memory_space=pltpu.HBM)
     dma = pltpu.SemaphoreType.DMA
     update, row_next, col_next = pl.pallas_call(
         functools.partial(soap_kernel, groups),
@@ -289,9 +309,13 @@
             jax.ShapeDtypeStruct((1, order), jnp.float32),
             jax.ShapeDtypeStruct((1, order), jnp.float32),
         ),
-        in_specs=[pl.BlockSpec(memory_space=pltpu.SMEM), vmem, hbm, hbm, hbm, hbm, vmem, vmem],
+        in_specs=[hbm] * 8,
         out_specs=(vmem, vmem, vmem),
         scratch_shapes=[
+            pltpu.SMEM((1, owners), jnp.int32),
+            pltpu.VMEM((owners, my_rows, order), jnp.bfloat16),
+            pltpu.VMEM((1, order), jnp.float32),
+            pltpu.VMEM((1, order), jnp.float32),
             pltpu.VMEM((2, order, order), jnp.bfloat16),
             pltpu.VMEM((2, order, order), jnp.bfloat16),
             pltpu.VMEM((owners, my_rows, order), jnp.bfloat16),
@@ -304,7 +328,7 @@
             pltpu.VMEM((2, order, order), jnp.float32),
             pltpu.VMEM((2, order, order), jnp.bfloat16),
             pltpu.VMEM((2, OUTER, 2 * OUTER), jnp.float32),
-            dma((4,)),
+            dma((owners + 7,)),
             dma((owners - 1,)),
             dma((owners - 1,)),
             dma((owners - 1,)),
@@ -319,9 +343,18 @@
         ),
         name="soap",
     )(
-        table, grad[0], left_stat[0, 0], right_stat[0, 0], left_basis[0, 0], right_basis[0, 0],
-        row_moment[0], col_moment[0],
+        *[pltpu.with_memory_space_constraint(v, pltpu.HBM) for v in (table, grad[0], left_stat[0, 0], right_stat[0, 0], left_basis[0, 0], right_basis[0, 0],
+        row_moment[0], col_moment[0])]
     )
+    update, row_next, col_next = pl.pallas_call(
+        store_kernel,
+        out_shape=tuple(jax.ShapeDtypeStruct(a.shape, a.dtype) for a in (update, row_next, col_next)),
+        in_specs=[vmem] * 3,
+        out_specs=[hbm] * 3,
+        scratch_shapes=[dma((3,))],
+        compiler_params=pltpu.CompilerParams(vmem_limit_bytes=4 * 1024 * 1024),
+        name="store",
+    )(update, row_next, col_next)
     return (update[None], row_next[None], col_next[None])
 
 

time: 60.2 us -> 52.3 us (0.87)
  local copies, waits for them, and re-layouts: 7.83 us -> 0 us
    unnamed x19 -> x0, local copies, waits for them, and re-layouts: 7.83 us -> none
    pallas_call x0 -> x1, Pallas kernels: none -> 0.83 us  [shards(): pl.pallas_call(store_kernel, out_shape=tuple((jax.ShapeDtypeStruct(a.shap...]
    pallas_call x1, Pallas kernels: 51.3 us -> 50.5 us  [shards(): pl.pallas_call(functools.partial(soap_kernel, groups), out_shape=(jax.Sha...]
where the time goes in v1:
time: 52.3 us; the launch traced here: 52.1 us
  Pallas kernels  51.3 us (98%)
  between operations  0.8 us (2%)
    pallas_call x1, Pallas kernels, shards(): pl.pallas_call(functools.partial(soap_kernel, groups), out_shape=(jax.Sha...  50.5 us

profile of v1, /device:TPU:0, one launch (start us, length us, event | category | flops | bytes accessed | tf_op | source)
XLA Modules:
  0.0 52.1 jit_solution(5027004043431301701)
XLA Ops:
  0.6 50.5 %soap.1 = (bf16[128,2048]{1,0:T(8,128)(2,1)S(1)}, f32[1,512]{1,0:T(1,128)S(1)}, f32[1,512]{1,0:T(1,128)S(1)}) custom-call(s32[1,4]{1,0:T(1,128)} %table_hbm.1, bf16[128,2048]{1,0:T(8,128)(2,1)} %bitcast.10, bf16[512,512]{1,0:T(8,128)(2,1)} %bitcast.11, bf16[512,512]{1,0:T(8,128)(2,1)} %bitcast.12, bf16[512,512]{1,0:T(8,128)(2,1)} %bitcast.13, ...), custom_call_target="tpu_custom_call" | custom-call | tf_op jit(solution)/shard_map/soap/pallas_call | solution.py:305
  51.1 0.8 %store.1 = (bf16[128,2048]{1,0:T(8,128)(2,1)}, f32[1,512]{1,0:T(1,128)}, f32[1,512]{1,0:T(1,128)}) custom-call(bf16[128,2048]{1,0:T(8,128)(2,1)S(1)} %get-tuple-element.9.update_ref, f32[1,512]{1,0:T(1,128)S(1)} %get-tuple-element.10.rn_ref, f32[1,512]{1,0:T(1,128)S(1)} %get-tuple-element.11.cn_ref), custom_call_target="tpu_custom_call" | custom-call | tf_op jit(solution)/shard_map/store/pallas_call | solution.py:349

commit v2 on v1

--- a/solution.py
+++ b/solution.py
@@ -10,9 +10,9 @@
 DECAY_MOMENT = 0.95
 CLIP_RMS = 0.5
 EPSILON = 1e-08
-OUTER = 128
-INNER = 32
+BLOCK = 64
 PANEL = 16
+SUB = 8
 
 NN = (((1,), (0,)), ((), ()))
 NT = (((1,), (1,)), ((), ()))
@@ -24,10 +24,6 @@
     return lax.dot_general(a, b, dims, preferred_element_type=jnp.float32)
 
 
-def mm_high(a, b, dims=NN):
-    return lax.dot_general(a, b, dims, preferred_element_type=jnp.float32, precision=lax.Precision.HIGHEST)
-
-
 def split(a):
     high = a.astype(jnp.bfloat16)
     return high, (a - high.astype(jnp.float32)).astype(jnp.bfloat16)
@@ -37,72 +33,178 @@
     return mm(a[0], b[0], dims) + (mm(a[0], b[1], dims) + mm(a[1], b[0], dims))
 
 
-def eliminate(pack):
-    lane = lax.broadcasted_iota(jnp.int32, pack.shape, 1)
-    row = lax.broadcasted_iota(jnp.int32, pack.shape, 0)
-    low = lane < 2 * INNER
-    scale = jnp.ones_like(pack)
+def spread(rows, column, sides):
+    low, high = (jnp.broadcast_to(rows[:, j : j + 1], rows.shape) for j in (column, BLOCK + column))
+    return jnp.where(sides[: rows.shape[0]], low, high)
+
+
+def invert(pack, pump):
+    shape = pack.shape
+    lane = lax.broadcasted_iota(jnp.int32, shape, 1)
+    row = lax.broadcasted_iota(jnp.int32, shape, 0)
+    sides = lane < BLOCK
+    local = jnp.where(sides, lane, lane - BLOCK)
+    top = row[:SUB]
     done = []
     rest = pack
-    for start in range(0, INNER, PANEL):
-        shape = rest.shape
-        below = lax.broadcasted_iota(jnp.int32, shape, 0)
-        half = low[: shape[0]]
-        columns = [
-            jnp.where(
-                half,
-                jnp.broadcast_to(rest[:, j : j + 1], shape),
-                jnp.broadcast_to(rest[:, 2 * INNER + j : 2 * INNER + j + 1], shape),
-            )
-            for j in range(start, start + PANEL)
-        ]
-        head_scale = jnp.ones((PANEL, shape[1]), jnp.float32)
+    for start in range(0, BLOCK, PANEL):
+        columns = [spread(rest[q // SUB * SUB :], start + q, sides) for q in range(PANEL)]
+        here = local[: rest.shape[0]] - start
+        unit = jnp.where(here == row[: rest.shape[0]], 1.0, 0.0)
+        rest = jnp.where((here >= 0) & (here < PANEL), unit, rest)
         for p in range(PANEL):
-            pivot = columns[p][p : p + 1, :]
+            s = p % SUB
+            column = columns[p]
+            pivot = column[s : s + 1]
+            inverse = 1.0 / pivot
             root = lax.rsqrt(pivot)
-            inverse = root * root
-            factor = jnp.where(below > p, columns[p], 0.0) * inverse
+            scale = jnp.where(top == s, root, 1.0 if s == 0 else scale)
+            factor = jnp.where(top > s, column[:SUB], 0.0)
+            if column.shape[0] > SUB:
+                factor = jnp.concatenate([factor, column[SUB:]], axis=0)
+            factor = factor * inverse
             for q in range(p + 1, PANEL):
-                columns[q] = columns[q] - factor * columns[q][p : p + 1, :]
-            rest = rest - factor * rest[p : p + 1, :]
-            head_scale = jnp.where(below[:PANEL] == p, root, head_scale)
-        done.append(rest[:PANEL] * head_scale)
-        rest = rest[PANEL:]
-    return jnp.concatenate(done, axis=0)
-
-
-def inverse_factors(grams, work):
-    row = lax.broadcasted_iota(jnp.int32, (OUTER, OUTER), 0)
-    col = lax.broadcasted_iota(jnp.int32, (OUTER, OUTER), 1)
-    eye = jnp.where(row == col, 1.0, 0.0)
+                m = q - p + s
+                part = factor if q // SUB == p // SUB else factor[SUB:]
+                columns[q] = columns[q] - part * column[m : m + 1]
+            rest = rest - factor * rest[s : s + 1]
+            if s == SUB - 1:
+                done.append(rest[:SUB] * scale)
+                rest = rest[SUB:]
+            pump()
+    return jnp.where(local <= row, jnp.concatenate(done, axis=0), 0.0)
+
+
+def twice(a):
+    return jnp.concatenate([a, a], axis=1)
+
+
+def swap(pieces):
+    return [pieces[i ^ 1] for i in range(len(pieces))]
+
+
+def orthonormalize(strip, x_ref, s_ref, xh_ref, xl_ref, o_ref, m_ref, q_ref, half_ref, g_ref):
+    order = x_ref.shape[-1]
+    blocks = order // BLOCK
+    group = 2 * BLOCK
+    lane = lax.broadcasted_iota(jnp.int32, (BLOCK, group), 1)
+    first = lane < BLOCK
+    queue = []
+
+    def pump(n=1):
+        for _ in range(min(n, len(queue))):
+            queue.pop(0)()
+
+    def flush():
+        pump(len(queue))
+
+    def gram_strip(c, t):
+        rows = pl.ds(t * group, group)
+        high, low = split(x_ref[c, rows, :])
+        xh_ref[c, rows, :] = high
+        xl_ref[c, rows, :] = low
+        width = (t + 1) * group
+        others = []
+        for ref in (xh_ref, xl_ref):
+            pieces = [ref[c, i * BLOCK : (i + 1) * BLOCK, :] for i in range(width // BLOCK)]
+            others.append(jnp.concatenate(swap(pieces) if c else pieces, axis=0))
+        s_ref[c, rows, :width] = mm_split((high, low), others, NT)
+
+    def lanes_of(b):
+        return slice(b // 2 * group, b // 2 * group + group)
+
+    def packed(b, rows):
+        pair = [s_ref[c, rows, lanes_of(b)] for c in range(2)]
+        keep = lax.broadcasted_iota(jnp.int32, pair[0].shape, 1) < BLOCK
+        return jnp.where(keep, pair[b % 2], pair[1 - b % 2])
+
     for c in range(2):
-        work[c, :, :OUTER] = grams[c]
-        work[c, :, OUTER:] = eye
-    small_row = lax.broadcasted_iota(jnp.int32, (INNER, OUTER), 0)
-    lane = lax.broadcasted_iota(jnp.int32, (INNER, OUTER), 1)
-    small_eye = jnp.where((lane == small_row + INNER) | (lane == small_row + 3 * INNER), 1.0, 0.0)
-    for b in range(OUTER // INNER):
-        rows = pl.ds(b * INNER, INNER)
-        left = work[0, rows, :OUTER]
-        right = work[1, rows, :OUTER]
-        if b:
-            left = pltpu.roll(left, OUTER - b * INNER, 1)
-        shift = (2 * INNER - b * INNER) % OUTER
-        if shift:
-            right = pltpu.roll(right, shift, 1)
-        pack = jnp.where(lane < INNER, left, small_eye)
-        pack = jnp.where((lane >= 2 * INNER) & (lane < 3 * INNER), right, pack)
-        pack = eliminate(pack)
+        strip(c, 0)
+        gram_strip(c, 0)
+    for t in range(1, order // group):
         for c in range(2):
-            factor = pltpu.roll(pack, OUTER - INNER if c == 0 else INNER, 1)[:, :INNER]
-            solved = mm_split(split(factor), split(work[c, rows, :]))
-            work[c, rows, :] = solved
-            if (b + 1) * INNER < OUTER:
-                tail = pl.ds((b + 1) * INNER, OUTER - (b + 1) * INNER)
-                high, low = split(solved)
-                cut = slice((b + 1) * INNER, OUTER)
-                work[c, tail, :] = work[c, tail, :] - mm_split((high[:, cut], low[:, cut]), (high, low), TN)
-    return [work[c, :, OUTER:] for c in range(2)]
+            queue.append(functools.partial(strip, c, t))
+            queue.append(functools.partial(gram_strip, c, t))
+    pack = packed(0, pl.ds(0, BLOCK))
+    for b in range(blocks):
+        inverse = invert(pack, functools.partial(pump, 1))
+        flush()
+        own = (first, ~first) if b % 2 == 0 else (~first, first)
+        sides = [jnp.where(own[c], inverse, 0.0) for c in range(2)]
+        weights = split(jnp.concatenate([sides[0], sides[0], sides[1], sides[1]], axis=0))
+
+        def panel(b, weights, start, stop):
+            rows = pl.ds(start, stop - start)
+            high, low = split(packed(b, rows))
+            o = mm(jnp.concatenate([high, low], axis=1), twice(weights[0]), NT) + mm(high, weights[1], NT)
+            high, low = split(o)
+            keep = lax.broadcasted_iota(jnp.int32, (stop - start, group), 1) < BLOCK
+            for c in range(2):
+                cut = slice(c * group, (c + 1) * group)
+                o_ref[c, rows, :] = jnp.concatenate([high[:, cut], low[:, cut]], axis=1)
+                mixed = jnp.where(keep, high[:, cut].astype(jnp.float32), low[:, cut].astype(jnp.float32)).astype(jnp.bfloat16)
+                for i in range(start // BLOCK, stop // BLOCK):
+                    place = (i ^ c) * BLOCK
+                    m_ref[c, place : place + BLOCK, :] = mixed[i * BLOCK - start : (i + 1) * BLOCK - start]
+
+        def trail(b, c, start, stop):
+            rows = pl.ds(start, stop - start)
+            near = (b + 1) // 2 * group
+            far = -(-stop // group) * group
+            cut = slice(near, far)
+            s_ref[c, rows, cut] = s_ref[c, rows, cut] - mm(o_ref[c, rows, :], twice(m_ref[c, near:far, :]), NT)
+
+        def finish(b, c, doubled):
+            rows = pl.ds(b * BLOCK, BLOCK)
+            high, low = split(x_ref[c, rows, :])
+            left = jnp.concatenate(split(doubled), axis=1)
+            q = mm(left, jnp.concatenate([high, low, high, low], axis=0))
+            high, low = split(q)
+            q_ref[c, rows, :] = high
+            xl_ref[c, rows, :] = low
+            if c == 0:
+                half_ref[rows, :] = mm(high, g_ref[...]).astype(jnp.bfloat16)
+
+        def deflate(b, c, start, stop):
+            rows = pl.ds(start, stop - start)
+            done = pl.ds(b * BLOCK, BLOCK)
+            high, low = q_ref[c, done, :], xl_ref[c, done, :]
+            x_ref[c, rows, :] = x_ref[c, rows, :] - mm(o_ref[c, rows, :], jnp.concatenate([high, low, high, low], axis=0))
+
+        near = (b + 1) * BLOCK
+        if near < order:
+            if b % 2 == 0:
+                for c in range(2):
+                    place = (b ^ c) * BLOCK
+                    m_ref[c, place : place + BLOCK, :] = jnp.zeros((BLOCK, group), jnp.bfloat16)
+            else:
+                for c in range(2):
+                    place = ((b + 2) ^ c) * BLOCK
+                    m_ref[c, place : place + BLOCK, :] = jnp.zeros((BLOCK, group), jnp.bfloat16)
+            panel(b, weights, near, near + BLOCK)
+            for c in range(2):
+                trail(b, c, near, near + BLOCK)
+            pack = packed(b + 1, pl.ds(near, BLOCK))
+        rolled = pltpu.roll(inverse, BLOCK, 1)
+        doubled = [jnp.where(own[c], inverse, rolled) for c in range(2)]
+        if near < order:
+            chunks = []
+            start = near + BLOCK
+            while start < order:
+                stop = min(order, start // group * group + group)
+                chunks.append((start, stop))
+                start = stop
+            for start, stop in chunks:
+                queue.append(functools.partial(panel, b, weights, start, stop))
+            for start, stop in chunks:
+                for c in range(2):
+                    queue.append(functools.partial(trail, b, c, start, stop))
+        for c in range(2):
+            queue.append(functools.partial(finish, b, c, doubled[c]))
+        for start, stop in ([(near, near + BLOCK)] + chunks) if near < order else []:
+            for c in range(2):
+                queue.append(functools.partial(deflate, b, c, start, stop))
+    flush()
 
 
 def partners(owners):
@@ -112,8 +214,8 @@
 def soap_kernel(
     groups, table_hbm, grad_hbm, ls_hbm, rs_hbm, lb_hbm, rb_hbm, rm_hbm, cm_hbm, out_ref, rn_ref, cn_ref,
     table_ref, grad_ref, rm_ref, cm_ref,
-    stat_ref, basis_ref, send_ref, block_ref, back_ref, ret_ref, sums_ref, totals_ref, part_ref,
-    x_ref, q_ref, work,
+    stat_ref, basis_ref, send_ref, block_ref, ret_ref, sums_ref, totals_ref, part_ref,
+    x_ref, q_ref, turned_ref, s_ref, xh_ref, xl_ref, o_ref, m_ref, half_ref,
     load_sem, stripe_send, stripe_recv, sum_send, sum_recv, total_send, total_recv, slab_send, slab_recv,
 ):
     owners, my_rows, order = send_ref.shape
@@ -188,7 +290,8 @@
         stripe_copies[-1].start()
     for copy in left:
         copy.wait()
-    x_ref[0] = mm(basis_ref[0], stat_ref[0], TN)
+    turned_ref[0] = basis_ref[0].T
+    x_ref[0] = mm(turned_ref[0], stat_ref[0])
     for copy in sum_copies:
         copy.wait_recv()
     matrix_sum = sums_ref[0]
@@ -209,11 +312,13 @@
             )
         )
         total_copies[-1].start()
-    x_ref[1] = mm(basis_ref[1], stat_ref[1], TN)
+    turned_ref[1] = basis_ref[1].T
+    x_ref[1] = mm(turned_ref[1], stat_ref[1])
     for copy in stripe_copies:
         copy.wait_recv()
     g = block_ref[...]
-    grams = [split(mm(g, g, dims)) for dims in (NT, TN)]
+    for c, dims in enumerate((NT, TN)):
+        stat_ref[c], basis_ref[c] = split(mm(g, g, dims))
     for copy in total_copies:
         copy.wait_recv()
     total = totals_ref[0]
@@ -222,27 +327,15 @@
     count = float(groups * owners * order * order)
     clip = (CLIP_RMS / jnp.sqrt(total / count + 1e-06))[:1, :1]
     weight = (1.0 - DECAY_STAT) * clip * clip
-    for c in range(2):
-        high, low = grams[c]
-        product = mm(basis_ref[c], high, TN) + mm(basis_ref[c], low, TN)
-        x_ref[c] = DECAY_STAT * x_ref[c] + weight * product
-    for k in range(order // OUTER):
-        rows = pl.ds(k * OUTER, OUTER)
-        grams = []
-        for c in range(2):
-            grams.append(mm_high(x_ref[c, rows, :], x_ref[c, rows, :], NT))
-        factors = inverse_factors(grams, work)
-        for c in range(2):
-            block = mm_split(split(factors[c]), split(x_ref[c, rows, :]))
-            q_ref[c, rows, :] = block.astype(jnp.bfloat16)
-            if (k + 1) * OUTER < order:
-                parts = split(block)
-                near, far = (k + 1) * OUTER, (k + 2) * OUTER
-                for tail in (pl.ds(near, OUTER), pl.ds(far, order - far)):
-                    if tail.size:
-                        along = mm_split(split(x_ref[c, tail, :]), parts, NT)
-                        x_ref[c, tail, :] = x_ref[c, tail, :] - mm_split(split(along), parts)
-    half = mm(q_ref[0], g).astype(jnp.bfloat16)
+
+    def strip(c, t):
+        rows = pl.ds(t * 2 * BLOCK, 2 * BLOCK)
+        left = turned_ref[c, rows, :]
+        product = mm(left, stat_ref[c]) + mm(left, basis_ref[c])
+        x_ref[c, rows, :] = DECAY_STAT * x_ref[c, rows, :] + weight * product
+
+    orthonormalize(strip, x_ref, s_ref, xh_ref, xl_ref, o_ref, m_ref, q_ref, half_ref, block_ref)
+    half = half_ref[...]
     rotated = clip * mm(half, q_ref[1], NT)
     square = rotated * rotated
     lanes = 128
@@ -254,13 +347,13 @@
     cn_ref[...] = col_next
     second = row_next.T[:, :1] * col_next / jnp.mean(row_next[:1])
     normed = (rotated / (jnp.sqrt(second) + EPSILON)).astype(jnp.bfloat16)
-    back_ref[...] = mm(q_ref[0], normed, TN).astype(jnp.bfloat16)
+    block_ref[...] = mm(q_ref[0], normed, TN).astype(jnp.bfloat16)
     for copy in stripe_copies:
         copy.wait_send()
 
     def slab(owner):
         rows = pl.ds(pl.multiple_of(owner * my_rows, my_rows), my_rows)
-        return mm(back_ref[rows, :], q_ref[1]).astype(jnp.bfloat16)
+        return mm(block_ref[rows, :], q_ref[1]).astype(jnp.bfloat16)
 
     for i, offset in enumerate(offsets):
         send_ref[peer(offset)] = slab(peer(offset))
@@ -320,14 +413,19 @@
             pltpu.VMEM((2, order, order), jnp.bfloat16),
             pltpu.VMEM((owners, my_rows, order), jnp.bfloat16),
             pltpu.VMEM((order, order), jnp.bfloat16),
-            pltpu.VMEM((order, order), jnp.bfloat16),
             pltpu.VMEM((owners, my_rows, order), jnp.bfloat16),
             pltpu.VMEM((owners, 8, 128), jnp.float32),
             pltpu.VMEM((groups, 8, 128), jnp.float32),
             pltpu.VMEM((2, 8, 128), jnp.float32),
             pltpu.VMEM((2, order, order), jnp.float32),
             pltpu.VMEM((2, order, order), jnp.bfloat16),
-            pltpu.VMEM((2, OUTER, 2 * OUTER), jnp.float32),
+            pltpu.VMEM((2, order, order), jnp.bfloat16),
+            pltpu.VMEM((2, order, order), jnp.float32),
+            pltpu.VMEM((2, order, order), jnp.bfloat16),
+            pltpu.VMEM((2, order, order), jnp.bfloat16),
+            pltpu.VMEM((2, order, 4 * BLOCK), jnp.bfloat16),
+            pltpu.VMEM((2, order, 2 * BLOCK), jnp.bfloat16),
+            pltpu.VMEM((order, order), jnp.bfloat16),
             dma((owners + 7,)),
             dma((owners - 1,)),
             dma((owners - 1,)),
@@ -339,7 +437,7 @@
             dma((owners - 1,)),
         ],
         compiler_params=pltpu.CompilerParams(
-            collective_id=0, has_side_effects=True, vmem_limit_bytes=48 * 1024 * 1024
+            collective_id=0, has_side_effects=True, vmem_limit_bytes=16 * 1024 * 1024 + 40 * order * order
         ),
         name="soap",
     )(

time: 52.3 us -> 41.6 us (0.80)
  Pallas kernels: 51.3 us -> 40.7 us
    pallas_call x1, Pallas kernels: 50.5 us -> 39.8 us  [shards(): pl.pallas_call(functools.partial(soap_kernel, groups), out_shape=(jax.Sha...]
where the time goes in v2:
time: 41.6 us; the launch traced here: 41.5 us
  Pallas kernels  40.7 us (98%)
  between operations  0.8 us (2%)
    pallas_call x1, Pallas kernels, shards(): pl.pallas_call(functools.partial(soap_kernel, groups), out_shape=(jax.Sha...  39.8 us

profile of v2, /device:TPU:0, one launch (start us, length us, event | category | flops | bytes accessed | tf_op | source)
XLA Modules:
  0.0 41.5 jit_solution(16599697172443046530)
XLA Ops:
  0.6 39.8 %soap.1 = (bf16[128,2048]{1,0:T(8,128)(2,1)S(1)}, f32[1,512]{1,0:T(1,128)S(1)}, f32[1,512]{1,0:T(1,128)S(1)}) custom-call(s32[1,4]{1,0:T(1,128)} %table_hbm.1, bf16[128,2048]{1,0:T(8,128)(2,1)} %bitcast.10, bf16[512,512]{1,0:T(8,128)(2,1)} %bitcast.11, bf16[512,512]{1,0:T(8,128)(2,1)} %bitcast.12, bf16[512,512]{1,0:T(8,128)(2,1)} %bitcast.13, ...), custom_call_target="tpu_custom_call" | custom-call | tf_op jit(solution)/shard_map/soap/pallas_call | solution.py:398
  40.5 0.8 %store.1 = (bf16[128,2048]{1,0:T(8,128)(2,1)}, f32[1,512]{1,0:T(1,128)}, f32[1,512]{1,0:T(1,128)}) custom-call(bf16[128,2048]{1,0:T(8,128)(2,1)S(1)} %get-tuple-element.9.update_ref, f32[1,512]{1,0:T(1,128)S(1)} %get-tuple-element.10.rn_ref, f32[1,512]{1,0:T(1,128)S(1)} %get-tuple-element.11.cn_ref), custom_call_target="tpu_custom_call" | custom-call | tf_op jit(solution)/shard_map/store/pallas_call | solution.py:447

commit v3 on v2

--- a/solution.py
+++ b/solution.py
@@ -11,7 +11,9 @@
 CLIP_RMS = 0.5
 EPSILON = 1e-08
 BLOCK = 64
-PANEL = 16
+TILE = 256
+RATE = 28
+PANELS = (8, 8, 16, 16, 16)
 SUB = 8
 
 NN = (((1,), (0,)), ((), ()))
@@ -47,31 +49,37 @@
     top = row[:SUB]
     done = []
     rest = pack
-    for start in range(0, BLOCK, PANEL):
-        columns = [spread(rest[q // SUB * SUB :], start + q, sides) for q in range(PANEL)]
+    start = 0
+    for width in PANELS:
+        columns = [spread(rest[q // SUB * SUB :], start + q, sides) for q in range(width)]
         here = local[: rest.shape[0]] - start
         unit = jnp.where(here == row[: rest.shape[0]], 1.0, 0.0)
-        rest = jnp.where((here >= 0) & (here < PANEL), unit, rest)
-        for p in range(PANEL):
+        rest = jnp.where((here >= 0) & (here < width), unit, rest)
+        for p in range(width):
             s = p % SUB
             column = columns[p]
             pivot = column[s : s + 1]
             inverse = 1.0 / pivot
             root = lax.rsqrt(pivot)
             scale = jnp.where(top == s, root, 1.0 if s == 0 else scale)
-            factor = jnp.where(top > s, column[:SUB], 0.0)
+            raw = jnp.where(top > s, column[:SUB], 0.0)
             if column.shape[0] > SUB:
-                factor = jnp.concatenate([factor, column[SUB:]], axis=0)
-            factor = factor * inverse
-            for q in range(p + 1, PANEL):
+                raw = jnp.concatenate([raw, column[SUB:]], axis=0)
+            factor = raw * inverse
+            for q in range(p + 1, width):
                 m = q - p + s
-                part = factor if q // SUB == p // SUB else factor[SUB:]
-                columns[q] = columns[q] - part * column[m : m + 1]
+                skip = 0 if q // SUB == p // SUB else SUB
+                taken = factor[skip:] * column[m : m + 1]
+                if q == p + 1:
+                    soon = raw[skip : skip + SUB] * column[m : m + 1] * inverse
+                    taken = jnp.concatenate([soon, taken[SUB:]], axis=0) if taken.shape[0] > SUB else soon
+                columns[q] = columns[q] - taken
             rest = rest - factor * rest[s : s + 1]
             if s == SUB - 1:
                 done.append(rest[:SUB] * scale)
                 rest = rest[SUB:]
             pump()
+        start += width
     return jnp.where(local <= row, jnp.concatenate(done, axis=0), 0.0)
 
 
@@ -83,27 +91,50 @@
     return [pieces[i ^ 1] for i in range(len(pieces))]
 
 
-def orthonormalize(strip, x_ref, s_ref, xh_ref, xl_ref, o_ref, m_ref, q_ref, half_ref, g_ref):
+def orthonormalize(strip, x_ref, s_ref, xh_ref, xl_ref, o_ref, m_ref, q_ref, half_ref, g_ref, turned_ref):
     order = x_ref.shape[-1]
     blocks = order // BLOCK
     group = 2 * BLOCK
     lane = lax.broadcasted_iota(jnp.int32, (BLOCK, group), 1)
     first = lane < BLOCK
     queue = []
-
-    def pump(n=1):
-        for _ in range(min(n, len(queue))):
-            queue.pop(0)()
-
-    def flush():
-        pump(len(queue))
-
-    def gram_strip(c, t):
-        rows = pl.ds(t * group, group)
+    last = blocks - 1
+
+    credit = [0]
+
+    def price(rows, depth, width, turned):
+        tiles = -(-depth // TILE) * -(-width // TILE)
+        return tiles * max(rows // 2, TILE // 2 if turned else TILE // 4) // 2
+
+    def later(deadline, cost, task, *arguments):
+        place = len(queue)
+        while place and queue[place - 1][0] > deadline:
+            place -= 1
+        queue.insert(place, (deadline, cost, functools.partial(task, *arguments)))
+
+    def run():
+        _, cost, task = queue.pop(0)
+        credit[0] -= cost
+        task()
+
+    def pump():
+        credit[0] = credit[0] + RATE
+        while queue and credit[0] >= 0:
+            run()
+        if not queue:
+            credit[0] = 0
+
+    def flush(deadline):
+        while queue and queue[0][0] <= deadline:
+            run()
+        credit[0] = 0
+
+    def gram_strip(c, start, stop):
+        rows = pl.ds(start, stop - start)
         high, low = split(x_ref[c, rows, :])
         xh_ref[c, rows, :] = high
         xl_ref[c, rows, :] = low
-        width = (t + 1) * group
+        width = stop
         others = []
         for ref in (xh_ref, xl_ref):
             pieces = [ref[c, i * BLOCK : (i + 1) * BLOCK, :] for i in range(width // BLOCK)]
@@ -120,39 +151,43 @@
 
     for c in range(2):
         strip(c, 0)
-        gram_strip(c, 0)
-    for t in range(1, order // group):
+        gram_strip(c, 0, group)
+    start = group
+    while start < order:
+        stop = min(start + (group if start == group else 2 * group), order)
         for c in range(2):
-            queue.append(functools.partial(strip, c, t))
-            queue.append(functools.partial(gram_strip, c, t))
+            for t in range(start // group, stop // group):
+                later(min(start // group, 2), 2 * price(group, order, order, False), strip, c, t)
+            later(min(start // group, 2), 3 * price(stop - start, order, stop, True), gram_strip, c, start, stop)
+        start = stop
     pack = packed(0, pl.ds(0, BLOCK))
     for b in range(blocks):
-        inverse = invert(pack, functools.partial(pump, 1))
-        flush()
+        inverse = invert(pack, pump)
+        flush(b)
         own = (first, ~first) if b % 2 == 0 else (~first, first)
         sides = [jnp.where(own[c], inverse, 0.0) for c in range(2)]
-        weights = split(jnp.concatenate([sides[0], sides[0], sides[1], sides[1]], axis=0))
+        weights = [split(jnp.concatenate([side, side], axis=0)) for side in sides]
 
         def panel(b, weights, start, stop):
             rows = pl.ds(start, stop - start)
             high, low = split(packed(b, rows))
-            o = mm(jnp.concatenate([high, low], axis=1), twice(weights[0]), NT) + mm(high, weights[1], NT)
-            high, low = split(o)
+            both = jnp.concatenate([high, low], axis=1)
             keep = lax.broadcasted_iota(jnp.int32, (stop - start, group), 1) < BLOCK
+            outs = [mm(both, twice(weights[c][0]), NT) + mm(both[:, :group], weights[c][1], NT) for c in range(2)]
             for c in range(2):
-                cut = slice(c * group, (c + 1) * group)
-                o_ref[c, rows, :] = jnp.concatenate([high[:, cut], low[:, cut]], axis=1)
-                mixed = jnp.where(keep, high[:, cut].astype(jnp.float32), low[:, cut].astype(jnp.float32)).astype(jnp.bfloat16)
+                high, low = split(outs[c])
+                o_ref[b % 2, c, rows, :] = jnp.concatenate([high, low], axis=1)
+                mixed = jnp.where(keep, high.astype(jnp.float32), low.astype(jnp.float32)).astype(jnp.bfloat16)
                 for i in range(start // BLOCK, stop // BLOCK):
                     place = (i ^ c) * BLOCK
-                    m_ref[c, place : place + BLOCK, :] = mixed[i * BLOCK - start : (i + 1) * BLOCK - start]
+                    m_ref[b % 2, c, place : place + BLOCK, :] = mixed[i * BLOCK - start : (i + 1) * BLOCK - start]
 
         def trail(b, c, start, stop):
             rows = pl.ds(start, stop - start)
             near = (b + 1) // 2 * group
             far = -(-stop // group) * group
             cut = slice(near, far)
-            s_ref[c, rows, cut] = s_ref[c, rows, cut] - mm(o_ref[c, rows, :], twice(m_ref[c, near:far, :]), NT)
+            s_ref[c, rows, cut] = s_ref[c, rows, cut] - mm(o_ref[b % 2, c, rows, :], twice(m_ref[b % 2, c, near:far, :]), NT)
 
         def finish(b, c, doubled):
             rows = pl.ds(b * BLOCK, BLOCK)
@@ -165,46 +200,50 @@
             if c == 0:
                 half_ref[rows, :] = mm(high, g_ref[...]).astype(jnp.bfloat16)
 
+        def turn(t):
+            rows = slice(t * group, (t + 1) * group)
+            turned_ref[:, rows] = q_ref[0, rows, :].T
+
         def deflate(b, c, start, stop):
             rows = pl.ds(start, stop - start)
             done = pl.ds(b * BLOCK, BLOCK)
             high, low = q_ref[c, done, :], xl_ref[c, done, :]
-            x_ref[c, rows, :] = x_ref[c, rows, :] - mm(o_ref[c, rows, :], jnp.concatenate([high, low, high, low], axis=0))
+            x_ref[c, rows, :] = x_ref[c, rows, :] - mm(o_ref[b % 2, c, rows, :], jnp.concatenate([high, low, high, low], axis=0))
 
         near = (b + 1) * BLOCK
         if near < order:
             if b % 2 == 0:
                 for c in range(2):
                     place = (b ^ c) * BLOCK
-                    m_ref[c, place : place + BLOCK, :] = jnp.zeros((BLOCK, group), jnp.bfloat16)
+                    m_ref[b % 2, c, place : place + BLOCK, :] = jnp.zeros((BLOCK, group), jnp.bfloat16)
             else:
                 for c in range(2):
                     place = ((b + 2) ^ c) * BLOCK
-                    m_ref[c, place : place + BLOCK, :] = jnp.zeros((BLOCK, group), jnp.bfloat16)
+                    m_ref[b % 2, c, place : place + BLOCK, :] = jnp.zeros((BLOCK, group), jnp.bfloat16)
             panel(b, weights, near, near + BLOCK)
             for c in range(2):
                 trail(b, c, near, near + BLOCK)
             pack = packed(b + 1, pl.ds(near, BLOCK))
         rolled = pltpu.roll(inverse, BLOCK, 1)
         doubled = [jnp.where(own[c], inverse, rolled) for c in range(2)]
+        chunks = []
+        middle = min(order, (near + BLOCK) // group * group + group)
+        for deadline, start, stop in ((b + 1, near + BLOCK, middle), (min(b + 2, last), middle, order)):
+            if start < stop:
+                chunks.append((deadline, start, stop))
+        for deadline, start, stop in chunks:
+            later(deadline, price(stop - start, 2 * TILE, TILE, True), panel, b, weights, start, stop)
+            for c in range(2):
+                later(deadline, price(stop - start, TILE, stop - near, True), trail, b, c, start, stop)
+        for c in range(2):
+            cost = price(BLOCK, TILE, order, False) + (price(BLOCK, order, order, False) if c == 0 else 0)
+            later(min(b + 2, last), cost, finish, b, c, doubled[c])
+        if b % 2:
+            later(min(b + 2, last), 0, turn, b // 2)
         if near < order:
-            chunks = []
-            start = near + BLOCK
-            while start < order:
-                stop = min(order, start // group * group + group)
-                chunks.append((start, stop))
-                start = stop
-            for start, stop in chunks:
-                queue.append(functools.partial(panel, b, weights, start, stop))
-            for start, stop in chunks:
-                for c in range(2):
-                    queue.append(functools.partial(trail, b, c, start, stop))
-        for c in range(2):
-            queue.append(functools.partial(finish, b, c, doubled[c]))
-        for start, stop in ([(near, near + BLOCK)] + chunks) if near < order else []:
             for c in range(2):
-                queue.append(functools.partial(deflate, b, c, start, stop))
-    flush()
+                later(min(b + 2, last), price(order - near, TILE, order, False), deflate, b, c, near, order)
+    flush(last)
 
 
 def partners(owners):
@@ -215,7 +254,7 @@
     groups, table_hbm, grad_hbm, ls_hbm, rs_hbm, lb_hbm, rb_hbm, rm_hbm, cm_hbm, out_ref, rn_ref, cn_ref,
     table_ref, grad_ref, rm_ref, cm_ref,
     stat_ref, basis_ref, send_ref, block_ref, ret_ref, sums_ref, totals_ref, part_ref,
-    x_ref, q_ref, turned_ref, s_ref, xh_ref, xl_ref, o_ref, m_ref, half_ref,
+    x_ref, q_ref, turned_ref, s_ref, xh_ref, xl_ref, o_ref, m_ref, half_ref, spare_ref, rows_ref,
     load_sem, stripe_send, stripe_recv, sum_send, sum_recv, total_send, total_recv, slab_send, slab_recv,
 ):
     owners, my_rows, order = send_ref.shape
@@ -314,6 +353,7 @@
         total_copies[-1].start()
     turned_ref[1] = basis_ref[1].T
     x_ref[1] = mm(turned_ref[1], stat_ref[1])
+    rows_ref[...] = jnp.broadcast_to(rm_ref[...], (rows_ref.shape[1], order)).T
     for copy in stripe_copies:
         copy.wait_recv()
     g = block_ref[...]
@@ -334,40 +374,41 @@
         product = mm(left, stat_ref[c]) + mm(left, basis_ref[c])
         x_ref[c, rows, :] = DECAY_STAT * x_ref[c, rows, :] + weight * product
 
-    orthonormalize(strip, x_ref, s_ref, xh_ref, xl_ref, o_ref, m_ref, q_ref, half_ref, block_ref)
+    orthonormalize(strip, x_ref, s_ref, xh_ref, xl_ref, o_ref, m_ref, q_ref, half_ref, block_ref, spare_ref)
     half = half_ref[...]
     rotated = clip * mm(half, q_ref[1], NT)
     square = rotated * rotated
-    lanes = 128
-    mean_row = jnp.broadcast_to(jnp.mean(square, axis=1, keepdims=True), (order, lanes))
-    mean_col = jnp.mean(square, axis=0, keepdims=True)
-    row_next = DECAY_MOMENT * jnp.broadcast_to(rm_ref[...], (lanes, order)) + (1.0 - DECAY_MOMENT) * mean_row.T
-    col_next = DECAY_MOMENT * cm_ref[...] + (1.0 - DECAY_MOMENT) * mean_col
-    rn_ref[...] = row_next[:1]
-    cn_ref[...] = col_next
-    second = row_next.T[:, :1] * col_next / jnp.mean(row_next[:1])
-    normed = (rotated / (jnp.sqrt(second) + EPSILON)).astype(jnp.bfloat16)
-    block_ref[...] = mm(q_ref[0], normed, TN).astype(jnp.bfloat16)
+    row_next = DECAY_MOMENT * rows_ref[...] + (1.0 - DECAY_MOMENT) * jnp.mean(square, axis=1, keepdims=True)
+    col_next = DECAY_MOMENT * cm_ref[...] + (1.0 - DECAY_MOMENT) * jnp.mean(square, axis=0, keepdims=True)
+    row_root = jnp.sqrt(row_next / jnp.mean(row_next, axis=0, keepdims=True))
+    spread_root = jnp.concatenate([row_root] * (order // row_root.shape[1]), axis=1)
+    normed = (rotated / (spread_root * jnp.sqrt(col_next) + EPSILON)).astype(jnp.bfloat16)
     for copy in stripe_copies:
         copy.wait_send()
 
-    def slab(owner):
+    def back(owner):
         rows = pl.ds(pl.multiple_of(owner * my_rows, my_rows), my_rows)
-        return mm(block_ref[rows, :], q_ref[1]).astype(jnp.bfloat16)
-
-    for i, offset in enumerate(offsets):
-        send_ref[peer(offset)] = slab(peer(offset))
+        return mm(spare_ref[rows, :], normed).astype(jnp.bfloat16)
+
+    targets = [peer(offset) for offset in offsets] + [me]
+    turned = back(targets[0])
+    for i, owner in enumerate(targets):
+        slab = mm(turned, q_ref[1]).astype(jnp.bfloat16)
+        if i == len(offsets):
+            ret_ref[me] = slab
+            break
+        send_ref[owner] = slab
+        turned = back(targets[i + 1])
         slab_copies.append(
             pltpu.make_async_remote_copy(
-                src_ref=send_ref.at[peer(offset)], dst_ref=ret_ref.at[me],
+                src_ref=send_ref.at[owner], dst_ref=ret_ref.at[me],
                 send_sem=slab_send.at[i], recv_sem=slab_recv.at[i],
-                device_id={"fsdp": peer(offset)}, device_id_type=MESH,
+                device_id={"fsdp": owner}, device_id_type=MESH,
             )
         )
-        if i:
-            slab_copies[i - 1].start()
-    ret_ref[me] = slab(me)
-    slab_copies[-1].start()
+        slab_copies[-1].start()
+    rn_ref[...] = row_next.T[:1]
+    cn_ref[...] = col_next
     for copy in slab_copies:
         copy.wait_recv()
     for j in range(owners):
@@ -423,9 +464,11 @@
             pltpu.VMEM((2, order, order), jnp.float32),
             pltpu.VMEM((2, order, order), jnp.bfloat16),
             pltpu.VMEM((2, order, order), jnp.bfloat16),
-            pltpu.VMEM((2, order, 4 * BLOCK), jnp.bfloat16),
-            pltpu.VMEM((2, order, 2 * BLOCK), jnp.bfloat16),
+            pltpu.VMEM((2, 2, order, 4 * BLOCK), jnp.bfloat16),
+            pltpu.VMEM((2, 2, order, 2 * BLOCK), jnp.bfloat16),
             pltpu.VMEM((order, order), jnp.bfloat16),
+            pltpu.VMEM((order, order), jnp.bfloat16),
+            pltpu.VMEM((order, 128), jnp.float32),
             dma((owners + 7,)),
             dma((owners - 1,)),
             dma((owners - 1,)),

time: 41.6 us -> 39.5 us (0.950)
  Pallas kernels: 40.7 us -> 38.6 us
    pallas_call x1, Pallas kernels: 39.8 us -> 37.8 us  [shards(): pl.pallas_call(functools.partial(soap_kernel, groups), out_shape=(jax.Sha...]
where the time goes in v3:
time: 39.5 us; the launch traced here: 39.4 us
  Pallas kernels  38.6 us (98%)
  between operations  0.8 us (2%)
    pallas_call x1, Pallas kernels, shards(): pl.pallas_call(functools.partial(soap_kernel, groups), out_shape=(jax.Sha...  37.8 us
    pallas_call x1, Pallas kernels, shards(): pl.pallas_call(store_kernel, out_shape=tuple((jax.ShapeDtypeStruct(a.shap...  0.83 us

profile of v3, /device:TPU:0, one launch (start us, length us, event | category | flops | bytes accessed | tf_op | source)
XLA Modules:
  0.0 39.4 jit_solution(9192148276647858353)
XLA Ops:
  0.6 37.8 %soap.1 = (bf16[128,2048]{1,0:T(8,128)(2,1)S(1)}, f32[1,512]{1,0:T(1,128)S(1)}, f32[1,512]{1,0:T(1,128)S(1)}) custom-call(s32[1,4]{1,0:T(1,128)} %table_hbm.1, bf16[128,2048]{1,0:T(8,128)(2,1)} %bitcast.10, bf16[512,512]{1,0:T(8,128)(2,1)} %bitcast.11, bf16[512,512]{1,0:T(8,128)(2,1)} %bitcast.12, bf16[512,512]{1,0:T(8,128)(2,1)} %bitcast.13, ...), custom_call_target="tpu_custom_call" | custom-call | tf_op jit(solution)/shard_map/soap/pallas_call | solution.py:439
  38.4 0.8 %store.1 = (bf16[128,2048]{1,0:T(8,128)(2,1)}, f32[1,512]{1,0:T(1,128)}, f32[1,512]{1,0:T(1,128)}) custom-call(bf16[128,2048]{1,0:T(8,128)(2,1)S(1)} %get-tuple-element.9.update_ref, f32[1,512]{1,0:T(1,128)S(1)} %get-tuple-element.10.rn_ref, f32[1,512]{1,0:T(1,128)S(1)} %get-tuple-element.11.cn_ref), custom_call_target="tpu_custom_call" | custom-call | tf_op jit(solution)/shard_map/store/pallas_call | solution.py:490

commit v4 on v3

--- a/solution.py
+++ b/solution.py
@@ -12,8 +12,9 @@
 EPSILON = 1e-08
 BLOCK = 64
 TILE = 256
-RATE = 28
-PANELS = (8, 8, 16, 16, 16)
+RATE = 22
+LAG = 3
+PANELS = (8, 8, 8, 8, 16, 16)
 SUB = 8
 
 NN = (((1,), (0,)), ((), ()))
@@ -150,15 +151,15 @@
         return jnp.where(keep, pair[b % 2], pair[1 - b % 2])
 
     for c in range(2):
-        strip(c, 0)
+        strip(c, 0, group)
         gram_strip(c, 0, group)
     start = group
     while start < order:
         stop = min(start + (group if start == group else 2 * group), order)
         for c in range(2):
-            for t in range(start // group, stop // group):
-                later(min(start // group, 2), 2 * price(group, order, order, False), strip, c, t)
-            later(min(start // group, 2), 3 * price(stop - start, order, stop, True), gram_strip, c, start, stop)
+            cost = price(stop - start, order, order, c == 1) + price(2 * (stop - start), order, order, c == 0)
+            later(1 if start == group else min(LAG, last), cost, strip, c, start, stop)
+            later(1 if start == group else min(LAG, last), 3 * price(stop - start, order, stop, True), gram_strip, c, start, stop)
         start = stop
     pack = packed(0, pl.ds(0, BLOCK))
     for b in range(blocks):
@@ -176,18 +177,18 @@
             outs = [mm(both, twice(weights[c][0]), NT) + mm(both[:, :group], weights[c][1], NT) for c in range(2)]
             for c in range(2):
                 high, low = split(outs[c])
-                o_ref[b % 2, c, rows, :] = jnp.concatenate([high, low], axis=1)
+                o_ref[b % LAG, c, rows, :] = jnp.concatenate([high, low], axis=1)
                 mixed = jnp.where(keep, high.astype(jnp.float32), low.astype(jnp.float32)).astype(jnp.bfloat16)
                 for i in range(start // BLOCK, stop // BLOCK):
                     place = (i ^ c) * BLOCK
-                    m_ref[b % 2, c, place : place + BLOCK, :] = mixed[i * BLOCK - start : (i + 1) * BLOCK - start]
+                    m_ref[b % LAG, c, place : place + BLOCK, :] = mixed[i * BLOCK - start : (i + 1) * BLOCK - start]
 
         def trail(b, c, start, stop):
             rows = pl.ds(start, stop - start)
             near = (b + 1) // 2 * group
             far = -(-stop // group) * group
             cut = slice(near, far)
-            s_ref[c, rows, cut] = s_ref[c, rows, cut] - mm(o_ref[b % 2, c, rows, :], twice(m_ref[b % 2, c, near:far, :]), NT)
+            s_ref[c, rows, cut] = s_ref[c, rows, cut] - mm(o_ref[b % LAG, c, rows, :], twice(m_ref[b % LAG, c, near:far, :]), NT)
 
         def finish(b, c, doubled):
             rows = pl.ds(b * BLOCK, BLOCK)
@@ -208,18 +209,18 @@
             rows = pl.ds(start, stop - start)
             done = pl.ds(b * BLOCK, BLOCK)
             high, low = q_ref[c, done, :], xl_ref[c, done, :]
-            x_ref[c, rows, :] = x_ref[c, rows, :] - mm(o_ref[b % 2, c, rows, :], jnp.concatenate([high, low, high, low], axis=0))
+            x_ref[c, rows, :] = x_ref[c, rows, :] - mm(o_ref[b % LAG, c, rows, :], jnp.concatenate([high, low, high, low], axis=0))
 
         near = (b + 1) * BLOCK
         if near < order:
             if b % 2 == 0:
                 for c in range(2):
                     place = (b ^ c) * BLOCK
-                    m_ref[b % 2, c, place : place + BLOCK, :] = jnp.zeros((BLOCK, group), jnp.bfloat16)
+                    m_ref[b % LAG, c, place : place + BLOCK, :] = jnp.zeros((BLOCK, group), jnp.bfloat16)
             else:
                 for c in range(2):
                     place = ((b + 2) ^ c) * BLOCK
-                    m_ref[b % 2, c, place : place + BLOCK, :] = jnp.zeros((BLOCK, group), jnp.bfloat16)
+                    m_ref[b % LAG, c, place : place + BLOCK, :] = jnp.zeros((BLOCK, group), jnp.bfloat16)
             panel(b, weights, near, near + BLOCK)
             for c in range(2):
                 trail(b, c, near, near + BLOCK)
@@ -228,7 +229,8 @@
         doubled = [jnp.where(own[c], inverse, rolled) for c in range(2)]
         chunks = []
         middle = min(order, (near + BLOCK) // group * group + group)
-        for deadline, start, stop in ((b + 1, near + BLOCK, middle), (min(b + 2, last), middle, order)):
+        due = min(b + LAG, max(b + 2, middle // BLOCK - 1), last)
+        for deadline, start, stop in ((b + 1, near + BLOCK, middle), (due, middle, order)):
             if start < stop:
                 chunks.append((deadline, start, stop))
         for deadline, start, stop in chunks:
@@ -237,12 +239,12 @@
                 later(deadline, price(stop - start, TILE, stop - near, True), trail, b, c, start, stop)
         for c in range(2):
             cost = price(BLOCK, TILE, order, False) + (price(BLOCK, order, order, False) if c == 0 else 0)
-            later(min(b + 2, last), cost, finish, b, c, doubled[c])
+            later(min(b + LAG, last), cost, finish, b, c, doubled[c])
         if b % 2:
-            later(min(b + 2, last), 0, turn, b // 2)
+            later(min(b + LAG, last), 0, turn, b // 2)
         if near < order:
             for c in range(2):
-                later(min(b + 2, last), price(order - near, TILE, order, False), deflate, b, c, near, order)
+                later(min(b + LAG, last), price(order - near, TILE, order, False), deflate, b, c, near, order)
     flush(last)
 
 
@@ -357,8 +359,14 @@
     for copy in stripe_copies:
         copy.wait_recv()
     g = block_ref[...]
-    for c, dims in enumerate((NT, TN)):
-        stat_ref[c], basis_ref[c] = split(mm(g, g, dims))
+
+    def inner(c, start, stop):
+        rows = pl.ds(start, stop - start)
+        through = split(mm(turned_ref[c, rows, :], g, NT if c else NN))
+        product = mm(jnp.concatenate(through, axis=0), g, NN if c else NT)
+        return product[: stop - start] + product[stop - start :]
+
+    heads = [inner(c, 0, 2 * BLOCK) for c in range(2)]
     for copy in total_copies:
         copy.wait_recv()
     total = totals_ref[0]
@@ -368,10 +376,9 @@
     clip = (CLIP_RMS / jnp.sqrt(total / count + 1e-06))[:1, :1]
     weight = (1.0 - DECAY_STAT) * clip * clip
 
-    def strip(c, t):
-        rows = pl.ds(t * 2 * BLOCK, 2 * BLOCK)
-        left = turned_ref[c, rows, :]
-        product = mm(left, stat_ref[c]) + mm(left, basis_ref[c])
+    def strip(c, start, stop):
+        rows = pl.ds(start, stop - start)
+        product = inner(c, start, stop) if start else heads[c]
         x_ref[c, rows, :] = DECAY_STAT * x_ref[c, rows, :] + weight * product
 
     orthonormalize(strip, x_ref, s_ref, xh_ref, xl_ref, o_ref, m_ref, q_ref, half_ref, block_ref, spare_ref)
@@ -464,8 +471,8 @@
             pltpu.VMEM((2, order, order), jnp.float32),
             pltpu.VMEM((2, order, order), jnp.bfloat16),
             pltpu.VMEM((2, order, order), jnp.bfloat16),
-            pltpu.VMEM((2, 2, order, 4 * BLOCK), jnp.bfloat16),
-            pltpu.VMEM((2, 2, order, 2 * BLOCK), jnp.bfloat16),
+            pltpu.VMEM((LAG, 2, order, 4 * BLOCK), jnp.bfloat16),
+            pltpu.VMEM((LAG, 2, order, 2 * BLOCK), jnp.bfloat16),
             pltpu.VMEM((order, order), jnp.bfloat16),
             pltpu.VMEM((order, order), jnp.bfloat16),
             pltpu.VMEM((order, 128), jnp.float32),

time: 39.5 us -> 38.8 us (0.982)
  Pallas kernels: 38.6 us -> 37.8 us
    pallas_call x1, Pallas kernels: 37.8 us -> 37 us  [shards(): pl.pallas_call(functools.partial(soap_kernel, groups), out_shape=(jax.Sha...]
where the time goes in v4:
time: 38.8 us; the launch traced here: 38.6 us
  Pallas kernels  37.8 us (97%)
  between operations  0.8 us (2%)
    pallas_call x1, Pallas kernels, shards(): pl.pallas_call(functools.partial(soap_kernel, groups), out_shape=(jax.Sha...  37 us
    pallas_call x1, Pallas kernels, shards(): pl.pallas_call(store_kernel, out_shape=tuple((jax.ShapeDtypeStruct(a.shap...  0.83 us

profile of v4, /device:TPU:0, one launch (start us, length us, event | category | flops | bytes accessed | tf_op | source)
XLA Modules:
  0.0 38.6 jit_solution(4517236174272795702)
XLA Ops:
  0.6 37.0 %soap.1 = (bf16[128,2048]{1,0:T(8,128)(2,1)S(1)}, f32[1,512]{1,0:T(1,128)S(1)}, f32[1,512]{1,0:T(1,128)S(1)}) custom-call(s32[1,4]{1,0:T(1,128)} %table_hbm.1, bf16[128,2048]{1,0:T(8,128)(2,1)} %bitcast.10, bf16[512,512]{1,0:T(8,128)(2,1)} %bitcast.11, bf16[512,512]{1,0:T(8,128)(2,1)} %bitcast.12, bf16[512,512]{1,0:T(8,128)(2,1)} %bitcast.13, ...), custom_call_target="tpu_custom_call" | custom-call | tf_op jit(solution)/shard_map/soap/pallas_call | solution.py:446
  37.6 0.8 %store.1 = (bf16[128,2048]{1,0:T(8,128)(2,1)}, f32[1,512]{1,0:T(1,128)}, f32[1,512]{1,0:T(1,128)}) custom-call(bf16[128,2048]{1,0:T(8,128)(2,1)S(1)} %get-tuple-element.9.update_ref, f32[1,512]{1,0:T(1,128)S(1)} %get-tuple-element.10.rn_ref, f32[1,512]{1,0:T(1,128)S(1)} %get-tuple-element.11.cn_ref), custom_call_target="tpu_custom_call" | custom-call | tf_op jit(solution)/shard_map/store/pallas_call | solution.py:497

commit v5 on v4

--- a/solution.py
+++ b/solution.py
@@ -12,7 +12,7 @@
 EPSILON = 1e-08
 BLOCK = 64
 TILE = 256
-RATE = 22
+RATE = 20
 LAG = 3
 PANELS = (8, 8, 8, 8, 16, 16)
 SUB = 8

time: 38.8 us -> 38.8 us (level)
  no operation moved by 1% of the time
where the time goes in v5:
time: 38.8 us; the launch traced here: 38.7 us
  Pallas kernels  37.9 us (98%)
  between operations  0.8 us (2%)
    pallas_call x1, Pallas kernels, shards(): pl.pallas_call(functools.partial(soap_kernel, groups), out_shape=(jax.Sha...  37 us
    pallas_call x1, Pallas kernels, shards(): pl.pallas_call(store_kernel, out_shape=tuple((jax.ShapeDtypeStruct(a.shap...  0.83 us

profile of v5, /device:TPU:0, one launch (start us, length us, event | category | flops | bytes accessed | tf_op | source)
XLA Modules:
  0.0 38.7 jit_solution(16374344804027319649)
XLA Ops:
  0.6 37.0 %soap.1 = (bf16[128,2048]{1,0:T(8,128)(2,1)S(1)}, f32[1,512]{1,0:T(1,128)S(1)}, f32[1,512]{1,0:T(1,128)S(1)}) custom-call(s32[1,4]{1,0:T(1,128)} %table_hbm.1, bf16[128,2048]{1,0:T(8,128)(2,1)} %bitcast.10, bf16[512,512]{1,0:T(8,128)(2,1)} %bitcast.11, bf16[512,512]{1,0:T(8,128)(2,1)} %bitcast.12, bf16[512,512]{1,0:T(8,128)(2,1)} %bitcast.13, ...), custom_call_target="tpu_custom_call" | custom-call | tf_op jit(solution)/shard_map/soap/pallas_call | solution.py:446
  37.7 0.8 %store.1 = (bf16[128,2048]{1,0:T(8,128)(2,1)}, f32[1,512]{1,0:T(1,128)}, f32[1,512]{1,0:T(1,128)}) custom-call(bf16[128,2048]{1,0:T(8,128)(2,1)S(1)} %get-tuple-element.9.update_ref, f32[1,512]{1,0:T(1,128)S(1)} %get-tuple-element.10.rn_ref, f32[1,512]{1,0:T(1,128)S(1)} %get-tuple-element.11.cn_ref), custom_call_target="tpu_custom_call" | custom-call | tf_op jit(solution)/shard_map/store/pallas_call | solution.py:497
